TPU v7x, 32 devices: a whole 2x2x4 slice. The times are simulated.
32 devices in a mesh: rep: 1, r: 4 (over z), s: 8 (over x, y, core).
Axes of the slice: x: 2, y: 2, z: 4, core: 2. Of those that a mesh axis runs over, the one named last changes fastest.
Arguments:
- x: bfloat16 [32, 4096, 768], P(('rep', 'r', 's'))
- dy: bfloat16 [32, 4096, 768], P(('rep', 'r', 's'))
- w_gate: bfloat16 [2, 768, 2304], P(None, 's')
- w_up: bfloat16 [2, 768, 2304], P(None, 's')
- w_down: bfloat16 [2, 2304, 768], P(None, 's')
Outputs:
- output 1: bfloat16 [32, 4096, 768], P(('rep', 'r', 's'))
- output 2: bfloat16 [2, 768, 2304], P('rep', 's')
- output 3: bfloat16 [2, 768, 2304], P('rep', 's')
- output 4: bfloat16 [2, 2304, 768], P('rep', 's')
All inputs are finite; a program needn't handle non-finite values.
Results may differ from a plain program's by a relative error of at most 0.018.
Values are sent between devices in bfloat16 or wider.
A program may use at most 2 GiB of HBM per device.

v0:
```python
import functools

import jax
import jax.numpy as jnp
from jax import lax
from jax.experimental import pallas as pl
from jax.experimental.pallas import tpu as pltpu
from jax.sharding import Mesh
from jax.sharding import PartitionSpec as P

BF, F32 = jnp.bfloat16, jnp.float32
TB = 512
CB = 768
NN, NT, TN = ((1,), (0,)), ((1,), (1,)), ((0,), (0,))
MESH = pl.DeviceIdType.MESH
DMA = pltpu.SemaphoreType.DMA


def dot(a, b, dims=NN):
    return lax.dot_general(a, b, (dims, ((), ())), preferred_element_type=F32)


def normed(h):
    wide = h.astype(F32)
    return (wide * lax.rsqrt(jnp.mean(wide**2, -1, keepdims=True) + 1e-6)).astype(BF)


def chip_peers():
    chip = lax.axis_index("chip")
    return chip + 1 - 2 * lax.rem(chip, 2), lax.rem(chip + 2, 4), 3 - chip


def z_peers():
    z = lax.axis_index("r")
    return z + 1 - 2 * lax.rem(z, 2), lax.rem(z + 2, 4)


def to_z(peer, **kw):
    return pltpu.make_async_remote_copy(device_id={"r": peer}, device_id_type=MESH, **kw)


def to_chip(peer, **kw):
    return pltpu.make_async_remote_copy(device_id={"chip": peer}, device_id_type=MESH, **kw)


def to_partner(**kw):
    return pltpu.make_async_remote_copy(device_id={"core": 1 - lax.axis_index("core")}, device_id_type=MESH, **kw)


def enter():
    barrier = pltpu.get_barrier_semaphore()
    for peer in chip_peers():
        pl.semaphore_signal(barrier, inc=1, device_id={"chip": peer}, device_id_type=MESH)
    pl.semaphore_signal(barrier, inc=1, device_id={"core": 1 - lax.axis_index("core")}, device_id_type=MESH)
    for peer in z_peers():
        pl.semaphore_signal(barrier, inc=1, device_id={"r": peer}, device_id_type=MESH)
    pl.semaphore_wait(barrier, 6)


class Gather:
    def __init__(self, *parts):
        self.rows, self.parts = parts[0][0].shape[1], parts
        self.ins = [(w, (1, *w.shape[1:]), lambda *_, l=l: (l, 0, 0)) for w, l, *_ in parts]
        self.outs = [((8 * self.rows, sum(p[3] for p in parts)), BF, None, None)]
        n = len(parts)
        self.scratch = [DMA((3, n)), DMA((3, n)), DMA((4, n)), DMA((4, n)), DMA((n,))]

    def bind(self, ins, outs, scratch):
        (self.full,) = outs
        chip, core = lax.axis_index("chip"), lax.axis_index("core")
        send, recv, psend, precv, local = scratch
        self.out, self.on, self.own, at = [], [], [], 0
        for k, (shard, (_, _, column, width)) in enumerate(zip(ins, self.parts)):

            def place(chip, core, at=at, width=width):
                first = pl.multiple_of((chip * 2 + core) * self.rows, self.rows)
                return self.full.at[pl.ds(first, self.rows), pl.ds(at, width)]

            mine, here = shard.at[0, :, pl.ds(column, width)], place(chip, core)
            self.own.append(to_partner(src_ref=mine, dst_ref=here, send_sem=psend.at[3, k], recv_sem=precv.at[3, k]))
            self.own.append(pltpu.make_async_copy(mine, here, local.at[k]))
            for i, peer in enumerate(chip_peers()):
                there = place(peer, core)
                self.out.append(to_chip(peer, src_ref=mine, dst_ref=here, send_sem=send.at[i, k], recv_sem=recv.at[i, k]))
                self.on.append(to_partner(src_ref=there, dst_ref=there, send_sem=psend.at[i, k], recv_sem=precv.at[i, k]))
            at += width

    def before(self, step, steps):
        if step == 0:
            for copy in self.out + self.own:
                copy.start()

    def after(self, step, steps):
        if step == steps - 1:
            self.forward()
            self.finish()

    def forward(self):
        for copy, on in zip(self.out, self.on):
            copy.wait_recv()
            on.start()

    def finish(self):
        for copy in self.out:
            copy.wait_send()
        for copy in self.on + self.own:
            copy.wait()


class Reduce:
    def __init__(self, source, *stages):
        self.stages, shape = stages, source.shape[-2:]
        self.ins = [(source, None, None)]
        self.outs = [(shape, BF, shape, lambda *_: (0, 0))]
        n = len(stages)
        self.scratch = [pltpu.VMEM((n, *shape), BF), DMA]
        for kind, _ in stages:
            k = 3 if kind == "chips" else 1
            self.scratch += [pltpu.VMEM((k, *shape), BF), DMA((k,)), DMA((k,))]

    def bind(self, ins, outs, scratch):
        (source,), (self.result,) = ins, outs
        self.own, local, *rest = scratch
        first = source.at[lax.axis_index("chip")] if self.stages[0][0] == "chips" else source
        self.load = pltpu.make_async_copy(first, self.own.at[0], local)
        self.copies, self.got = [], []
        for j, (kind, _) in enumerate(self.stages):
            got, send, recv = rest[3 * j : 3 * j + 3]
            self.got.append(got)
            if kind == "chips":
                self.copies.append(
                    [
                        to_chip(peer, src_ref=source.at[peer], dst_ref=got.at[i], send_sem=send.at[i], recv_sem=recv.at[i])
                        for i, peer in enumerate(chip_peers())
                    ]
                )
            else:
                here = source if j == 0 else self.own.at[j]
                self.copies.append([to_z(z_peers()[kind], src_ref=here, dst_ref=got.at[0], send_sem=send.at[0], recv_sem=recv.at[0])])

    def add(self, j):
        if j == 0:
            self.load.wait()
        for copy in self.copies[j]:
            copy.wait()
        total = self.own[j].astype(F32)
        for i in range(len(self.copies[j])):
            total += self.got[j][i].astype(F32)
        if j + 1 < len(self.stages):
            self.own[j + 1] = total.astype(BF)
        else:
            self.result[...] = total.astype(BF)

    def before(self, step, steps):
        if step == 0:
            self.load.start()
            for copy in self.copies[0]:
                copy.start()
        for j, (_, when) in enumerate(self.stages):
            if when == step:
                self.add(j)

    def after(self, step, steps):
        for j, (_, when) in enumerate(self.stages):
            if when == step:
                for copy in self.copies[j + 1]:
                    copy.start()
            if when is None and step == steps - 1:
                self.add(j)


def pair_sum(acc, sums_ref, sent, got, send, recv):
    core = lax.axis_index("core")
    chips, rows = sums_ref.shape[:2]

    def rows_of(chip, core):
        return acc[pl.ds(pl.multiple_of((chip * 2 + core) * rows, rows), rows), :]

    for chip in range(chips):
        sent[chip] = rows_of(chip, 1 - core).astype(BF)
    copy = to_partner(src_ref=sent, dst_ref=got, send_sem=send, recv_sem=recv)
    copy.start()
    copy.wait()
    for chip in range(chips):
        sums_ref[chip] = (rows_of(chip, core) + got[chip].astype(F32)).astype(BF)


def pair_scratch(rows, n):
    return [pltpu.VMEM((4, rows, n), BF)] * 2 + [DMA, DMA]


def call(kernel, grid, ins, outs, scratch, flops, number, moves=(), aliases=None, steered=False, name=None):
    def spec(block, index):
        return pl.BlockSpec(memory_space=pl.ANY) if block is None else pl.BlockSpec(block, index)

    n_in, n_out, n_scratch = len(ins), len(outs), len(scratch)
    all_ins = list(ins) + [a for m in moves for a in m.ins]
    all_outs = list(outs) + [a for m in moves for a in m.outs]
    all_scratch = list(scratch) + [a for m in moves for a in m.scratch]

    def body(*refs):
        ins_, outs_, scratch_ = refs[: len(all_ins)], refs[len(all_ins) : len(all_ins) + len(all_outs)], refs[len(all_ins) + len(all_outs) :]
        i, o, c = n_in, n_out, n_scratch
        for m in moves:
            m.bind(ins_[i : i + len(m.ins)], outs_[o : o + len(m.outs)], scratch_[c : c + len(m.scratch)])
            i, o, c = i + len(m.ins), o + len(m.outs), c + len(m.scratch)
        if number is not None:

            @pl.when(functools.reduce(lambda a, b: a & b, [pl.program_id(k) == 0 for k in range(len(grid))]))
            def _():
                enter()

        if steered or not moves:
            kernel(*ins_[:n_in], *outs_[:n_out], *scratch_[:n_scratch], *moves)
            return

        def at_steps(do):
            for step in steps:

                @pl.when(pl.program_id(0) == step)
                def _():
                    for m in moves:
                        getattr(m, do)(step, grid[0])

        steps = sorted({0, grid[0] - 1} | {when for m in moves for _, when in getattr(m, "stages", ()) if when is not None})
        at_steps("before")
        kernel(*ins_[:n_in], *outs_[:n_out], *scratch_[:n_scratch])
        at_steps("after")

    size = sum(a.size * a.dtype.itemsize for a, *_ in ins)
    return pl.pallas_call(
        body,
        grid=grid,
        in_specs=[spec(b, i) for _, b, i in all_ins],
        out_specs=[spec(b, i) for *_, b, i in all_outs],
        out_shape=[jax.ShapeDtypeStruct(s, d) for s, d, *_ in all_outs],
        scratch_shapes=all_scratch,
        input_output_aliases=aliases or {},
        cost_estimate=pl.CostEstimate(flops=flops, bytes_accessed=size, transcendentals=0),
        compiler_params=pltpu.CompilerParams(
            vmem_limit_bytes=62 * 2**20,
            dimension_semantics=("arbitrary",) * len(grid),
            collective_id=number,
            has_side_effects=number is not None,
        ),
        name=name,
    )(*[a for a, *_ in all_ins])


def fwd_kernel(x_ref, gate_ref, up_ref, p_ref, a_ref, h_ref, a2_ref, w, wd, a_all, p_all, local, *moves):
    c, t = pl.program_id(0), pl.program_id(1)
    nt, nc = pl.num_programs(1), len(moves) - 3
    late = 2

    def fetch(full, to):
        copy = pltpu.make_async_copy(full, to, local)
        copy.start()
        copy.wait()

    for i, move in enumerate(moves):

        @pl.when((c == 0) & (t == 0))
        def _():
            move.before(0, 1)
            if i == 0:
                move.forward()

        if 0 < i <= nc:

            @pl.when((c == i - 1) & (t == nt - late))
            def _():
                move.forward()

        if i <= nc:

            @pl.when((c == i) & (t == 0))
            def _():
                move.finish()
                fetch(move.full, w if i < nc else wd)

    rows = pl.ds(pl.multiple_of(t * TB, TB), TB)

    @pl.when(c == 0)
    def _():
        a = normed(x_ref[...])
        a_ref[...] = a
        a_all[rows, :] = a

    @pl.when(c < nc)
    def _():
        a = a_all[rows, :]
        gate, up = dot(a, w[:, :CB]), dot(a, w[:, CB:])
        gate_ref[...], up_ref[...] = gate, up
        p = (gate * jax.nn.sigmoid(gate) * up).astype(BF)
        p_ref[...] = p
        p_all[jnp.minimum(c, nc - 1), rows, :] = p

    @pl.when(c == nc)
    def _():
        h = x_ref[...] + sum(dot(p_all[i, rows, :], wd[i * CB : (i + 1) * CB, :]) for i in range(nc)).astype(BF)
        h_ref[...] = h
        a2_ref[...] = normed(h)

        @pl.when(t == nt - 1)
        def _():
            for move in moves[nc + 1 :]:
                move.forward()
            for move in moves[nc + 1 :]:
                move.finish()


def back_kernel(saved, n_alias, *refs):
    refs = list(refs)
    a_ref, dh_ref, wd_ref = refs[:3]
    given = refs[3:5] if saved else refs[3:4]
    refs = refs[3 + len(given) + n_alias :]
    d_ref = refs.pop(0)
    p_ref = None if saved else refs.pop(0)
    sums_ref, acc, *pair = refs
    t = pl.program_id(0)

    @pl.when(t == 0)
    def _():
        acc[...] = jnp.zeros_like(acc)

    a, dh = a_ref[...], dh_ref[...]
    if saved:
        gate, up = given[0][...], given[1][...]
    else:
        gate, up = dot(a, given[0][:, :CB]), dot(a, given[0][:, CB:])
    dp = dot(dh, wd_ref[...], NT).astype(BF).astype(F32)
    sig = jax.nn.sigmoid(gate)
    silu = gate * sig
    d_ref[:, :CB] = (dp * up * (sig + silu * (1 - sig))).astype(BF)
    d_ref[:, CB:] = (dp * silu).astype(BF)
    if not saved:
        p_ref[...] = (silu * up).astype(BF)
    acc[...] += dot(a, d_ref[...], TN)

    @pl.when(t == pl.num_programs(0) - 1)
    def _():
        pair_sum(acc, sums_ref, *pair)


def down_back_kernel(p_ref, dh_ref, sums_ref, acc, *pair):
    t = pl.program_id(0)

    @pl.when(t == 0)
    def _():
        acc[...] = jnp.zeros_like(acc)

    acc[...] += dot(p_ref[...], dh_ref[...], TN)

    @pl.when(t == pl.num_programs(0) - 1)
    def _():
        pair_sum(acc, sums_ref, *pair)


def input_back_kernel(d_ref, h_ref, dh_ref, *refs):
    *weights, out_ref = refs
    da = sum(dot(d_ref[:, 2 * CB * c : 2 * CB * (c + 1)], w[...], NT) for c, w in enumerate(weights)).astype(BF)
    g, h = da.astype(F32), h_ref[...].astype(F32)
    scale = lax.rsqrt(jnp.mean(h**2, -1, keepdims=True) + 1e-6)
    dn = g * scale - h * (scale**3 * jnp.mean(g * h, -1, keepdims=True))
    out_ref[...] = dh_ref[...] + dn.astype(BF)


def stack_kernel(*refs):
    *chunks, d0, d1, dg, du, dd = refs
    nc = len(chunks) // 2
    for i, ref in enumerate(chunks):
        at = slice(i % nc * CB, (i % nc + 1) * CB)
        dg[i // nc, :, at] = ref[:, :CB]
        du[i // nc, :, at] = ref[:, CB:]
    dd[0], dd[1] = d0[...], d1[...]


def solution(mesh):
    sizes = mesh.shape
    rep, r, s = sizes["rep"], sizes["r"], sizes["s"]
    fine = Mesh(mesh.devices.reshape(rep, r, s // 2, 2), ("rep", "r", "chip", "core"))

    def step(x, dy, w_gate, w_up, w_down):
        x, dy = x[0], dy[0]
        tokens, d = x.shape
        layers, _, ff = w_gate.shape
        nt, nc = tokens // TB, ff // CB
        row = lambda t: (t, 0)
        rows_d, rows_f = d // s, ff // s
        mm = 2 * tokens * d * ff
        blockrow = (TB, d)
        state = ((tokens, d), BF, blockrow, row)
        numbers = iter(range(100))

        def chunk(l, c):
            return Gather((w_gate, l, c * CB, CB), (w_up, l, c * CB, CB))

        def down(l):
            return Gather((w_down, l, 0, d))

        first = lambda c, t: (jnp.where(c == 0, t, nt - 1), 0)
        ends = lambda c, t: (jnp.where((c == 0) | (c == nc), t, nt - 1), 0)
        then = lambda c, t: (jnp.where(c == nc, t, 0), 0)
        chunked = lambda c, t: (jnp.where(c < nc, t, nt - 1), jnp.minimum(c, nc - 1))
        gate, up, p1, a1, h1, a2, *full = call(
            fwd_kernel,
            (nc + 1, nt),
            [(x, blockrow, ends)],
            [((tokens, ff), dt, (TB, CB), chunked) for dt in (F32, F32, BF)] + [((tokens, d), BF, blockrow, i) for i in (first, then, then)],
            [pltpu.VMEM((d, 2 * CB), BF), pltpu.VMEM((ff, d), BF), pltpu.VMEM((tokens, d), BF), pltpu.VMEM((nc, tokens, CB), BF), DMA],
            3 * mm,
            next(numbers),
            [chunk(0, c) for c in range(nc)] + [down(0), down(1), chunk(1, 0)],
            steered=True,
            name="fwd",
        )
        gu1, (wd1, wd2, gu2_0) = full[:nc], full[nc:]

        def back(c, a, dh, wd, so_far, moves, w=None):
            here = lambda t: (t, c)
            ins = [(a, blockrow, row), (dh, blockrow, row), (wd, (CB, d), lambda t: (c, 0))]
            outs = [((tokens, 2 * ff), BF, (TB, 2 * CB), here)]
            if w is None:
                ins += [(gate, (TB, CB), here), (up, (TB, CB), here)]
            else:
                ins += [(w, (d, 2 * CB), lambda t: (0, 0))]
                outs += [((tokens, ff), BF, (TB, CB), here)]
            aliases = {len(ins) + i: i for i in range(len(so_far))}
            ins += [(buffer, None, None) for buffer in so_far]
            n = len(outs)
            outs += [((4, rows_d, 2 * CB), BF, (4, rows_d, 2 * CB), lambda t: (0, 0, 0))]
            got = call(
                functools.partial(back_kernel, w is None, len(so_far)),
                (nt,),
                ins,
                outs,
                [pltpu.VMEM((d, 2 * CB), F32)] + pair_scratch(rows_d, 2 * CB),
                (3 if w is None else 5) * mm // nc,
                next(numbers),
                moves,
                aliases,
                name="back",
            )
            return got[:n], got[n], got[n + 1 :]

        def down_back(p, dh, moves):
            return call(
                down_back_kernel,
                (nt,),
                [(p, (TB, ff), row), (dh, blockrow, row)],
                [((4, rows_f, d), BF, (4, rows_f, d), lambda t: (0, 0, 0))],
                [pltpu.VMEM((ff, d), F32)] + pair_scratch(rows_f, d),
                mm,
                next(numbers),
                moves,
                name="down_back",
            )

        def input_back(dgu, h, dh, ws, moves=()):
            return call(
                input_back_kernel,
                (nt,),
                [(dgu, (TB, 2 * ff), row), (h, blockrow, row), (dh, blockrow, row)] + [(w, w.shape, lambda t: (0, 0)) for w in ws],
                [state],
                [],
                2 * mm,
                next(numbers) if moves else None,
                moves,
                name="input_back",
            )

        so_far, s20, (gu2_1, gu2_2) = back(0, a2, dy, wd2, [], [chunk(1, 1), chunk(1, 2)], gu2_0)
        so_far, s21, (u20,) = back(1, a2, dy, wd2, so_far, [Reduce(s20, ("chips", None))], gu2_1)
        (dgu2, p2), s22, (t20, u21) = back(
            2, a2, dy, wd2, so_far, [Reduce(u20, (0, 3), (1, None)), Reduce(s21, ("chips", None))], gu2_2
        )
        s2d, t21, u22 = down_back(p2, dy, [Reduce(u21, (0, 3), (1, None)), Reduce(s22, ("chips", None))])
        dh1, t22, u2d = input_back(dgu2, h1, dy, [gu2_0, gu2_1, gu2_2], [Reduce(u22, (0, 3), (1, None)), Reduce(s2d, ("chips", None))])
        s1d, v2d = down_back(p1, dh1, [Reduce(u2d, (0, None))])
        so_far, s10, (t2d, u1d) = back(0, a1, dh1, wd1, [], [Reduce(v2d, (1, None)), Reduce(s1d, ("chips", None))])
        so_far, s11, (v1d, u10) = back(1, a1, dh1, wd1, so_far, [Reduce(u1d, (0, None)), Reduce(s10, ("chips", None))])
        (dgu1,), s12, (t1d, v10, u11) = back(
            2, a1, dh1, wd1, so_far, [Reduce(v1d, (1, None)), Reduce(u10, (0, None)), Reduce(s11, ("chips", None))]
        )
        dx, t10, t11, t12 = input_back(
            dgu1, x, dh1, gu1, [Reduce(v10, (1, None)), Reduce(u11, (0, 2), (1, None)), Reduce(s12, ("chips", 3), (0, 5), (1, None))]
        )

        w_out = [((layers, rows_d, ff), BF)] * 2 + [((layers, rows_f, d), BF)]
        terms = (t10, t11, t12, t20, t21, t22, t1d, t2d)
        dg, du, dd = call(
            stack_kernel,
            (1,),
            [(t, t.shape, lambda _: (0, 0)) for t in terms],
            [(shape, dt, shape, lambda _: (0, 0, 0)) for shape, dt in w_out],
            [],
            10**6,
            None,
            name="stack",
        )
        return dx[None], dg, du, dd

    states, cut = P(("rep", "r", "chip", "core"), None, None), P(None, ("chip", "core"), None)
    return jax.shard_map(
        step,
        mesh=fine,
        in_specs=(states, states) + (cut,) * 3,
        out_specs=(states,) + (P("rep", ("chip", "core"), None),) * 3,
        check_vma=False,
    )
```

profile of v0, /device:TPU:0, one launch (start us, length us, event | category | flops | bytes accessed | tf_op | source)
XLA Modules:
  0.0 492.8 jit_solution(11643241766511426229)
XLA Ops:
  0.6 108.3 %fwd.1 = (f32[4096,2304]{1,0:T(8,128)}, f32[4096,2304]{1,0:T(8,128)}, bf16[4096,2304]{1,0:T(8,128)(2,1)}, bf16[4096,768]{1,0:T(8,128)(2,1)}, bf16[4096,768]{1,0:...) custom-call(bf16[4096,768]{1,0:T(8,128)(2,1)} %bitcast.9, ...), custom_call_target="tpu_custom_call" | custom-call | flops 43486543872 | bytes 6291456 | tf_op jit(solution)/shard_map/fwd/pallas_call | solution.py:231
  108.9 44.5 %back.6 = (bf16[4096,4608]{1,0:T(8,128)(2,1)}, bf16[4096,2304]{1,0:T(8,128)(2,1)}, bf16[4,96,1536]{2,1,0:T(8,128)(2,1)}, bf16[768,1536]{1,0:T(8,128)(2,1)}, bf16[768,1536]{1,0:T(8,128)(2,1)}) custom-call(bf16[4096,768]{1,0:T(8,128)(2,1)} %get-tuple-element.59.refs_0_, bf16[4096,768]{1,0:T(8,128)(2,1)} %bitcast.4, ...), custom_call_target="tpu_custom_call" | custom-call | flops 24159191040 | bytes 18481152 | tf_op jit(solution)/shard_map/back/pallas_call | solution.py:231
  153.5 38.3 %back.7 = (bf16[4096,4608]{1,0:T(8,128)(2,1)}, bf16[4096,2304]{1,0:T(8,128)(2,1)}, bf16[4,96,1536]{2,1,0:T(8,128)(2,1)}, bf16[96,1536]{1,0:T(8,128)(2,1)}) custom-call(bf16[4096,768]{1,0:T(8,128)(2,1)} %get-tuple-element.59.refs_0_, bf16[4096,768]{1,0:T(8,128)(2,1)} %bitcast.5, ...), custom_call_target="tpu_custom_call", output_to_operand_aliasing={{0}: (4, {}), {1}: (5, {})} | custom-call | flops 24159191040 | bytes 75104256 | tf_op jit(solution)/shard_map/back/pallas_call | solution.py:231
  191.7 38.4 %back.8 = (bf16[4096,4608]{1,0:T(8,128)(2,1)}, bf16[4096,2304]{1,0:T(8,128)(2,1)}, bf16[4,96,1536]{2,1,0:T(8,128)(2,1)}, bf16[96,1536]{1,0:T(8,128)(2,1)}, bf16[96,1536]{1,0:T(8,128)(2,1)}) custom-call(bf16[4096,768]{1,0:T(8,128)(2,1)} %get-tuple-element.59.refs_0_, bf16[4096,768]{1,0:T(8,128)(2,1)} %bitcast.6, ...), custom_call_target="tpu_custom_call", output_to_operand_aliasing={{0}: (4, {}), {1}: (5, {})} | custom-call | flops 24159191040 | bytes 75104256 | tf_op jit(solution)/shard_map/back/pallas_call | solution.py:231
  230.1 30.4 %down_back.2 = (bf16[4,288,768]{2,1,0:T(8,128)(2,1)}, bf16[96,1536]{1,0:T(8,128)(2,1)}, bf16[96,1536]{1,0:T(8,128)(2,1)}) custom-call(bf16[4096,2304]{1,0:T(8,128)(2,1)} %get-tuple-element.73.refs_0_, bf16[4096,768]{1,0:T(8,128)(2,1)} %bitcast.7, bf16[96,1536]{1,0:T(8,128)(2,1)} %get-tuple-element.74.refs_2_, bf16[4,96,1536]{2,1,0:T(8,128)(2,1)} %get-tuple-element.75.refs_3_), custom_call_target="tpu_custom_call" | custom-call | flops 14495514624 | bytes 25165824 | tf_op jit(solution)/shard_map/down_back/pallas_call | solution.py:231
  260.5 41.7 %input_back.2 = (bf16[4096,768]{1,0:T(8,128)(2,1)}, bf16[96,1536]{1,0:T(8,128)(2,1)}, bf16[288,768]{1,0:T(8,128)(2,1)}) custom-call(bf16[4096,4608]{1,0:T(8,128)(2,1)} %get-tuple-element.71.refs_0_, bf16[4096,768]{1,0:T(8,128)(2,1)} %get-tuple-element.72.refs_1_, bf16[4096,768]{1,0:T(8,128)(2,1)} %bitcast.8, bf16[768,1536]{1,0:T(8,128)(2,1)} %get-tuple-element.61.refs_3_, ...), custom_call_target="tpu_custom_call" | custom-call | flops 28991029248 | bytes 57409536 | tf_op jit(solution)/shard_map/input_back/pallas_call | solution.py:231
  302.2 26.4 %down_back.3 = (bf16[4,288,768]{2,1,0:T(8,128)(2,1)}, bf16[288,768]{1,0:T(8,128)(2,1)}) custom-call(bf16[4096,2304]{1,0:T(8,128)(2,1)} %get-tuple-element.82.refs_0_, bf16[4096,768]{1,0:T(8,128)(2,1)} %get-tuple-element.78.refs_1_.refs_2_, bf16[288,768]{1,0:T(8,128)(2,1)} %get-tuple-element.83.refs_2_), custom_call_target="tpu_custom_call" | custom-call | flops 14495514624 | bytes 25165824 | tf_op jit(solution)/shard_map/down_back/pallas_call | solution.py:231
  328.5 30.5 %back.9 = (bf16[4096,4608]{1,0:T(8,128)(2,1)}, bf16[4,96,1536]{2,1,0:T(8,128)(2,1)}, bf16[288,768]{1,0:T(8,128)(2,1)}, bf16[288,768]{1,0:T(8,128)(2,1)}) custom-call(bf16[4096,768]{1,0:T(8,128)(2,1)} %get-tuple-element.58.refs_0_, bf16[4096,768]{1,0:T(8,128)(2,1)} %get-tuple-element.78.refs_1_.refs_2_, bf16[2304,768]{1,0:T(8,128)(2,1)} %get-tuple-element.79.refs_2_, ...), custom_call_target="tpu_custom_call" | custom-call | flops 14495514624 | bytes 91619328 | tf_op jit(solution)/shard_map/back/pallas_call | solution.py:231
  359.1 31.0 %back.10 = (bf16[4096,4608]{1,0:T(8,128)(2,1)}, bf16[4,96,1536]{2,1,0:T(8,128)(2,1)}, bf16[288,768]{1,0:T(8,128)(2,1)}, bf16[96,1536]{1,0:T(8,128)(2,1)}) custom-call(bf16[4096,768]{1,0:T(8,128)(2,1)} %get-tuple-element.58.refs_0_, bf16[4096,768]{1,0:T(8,128)(2,1)} %get-tuple-element.78.refs_1_.refs_2_, ...), custom_call_target="tpu_custom_call", output_to_operand_aliasing={{0}: (5, {})} | custom-call | flops 14495514624 | bytes 129368064 | tf_op jit(solution)/shard_map/back/pallas_call | solution.py:231
  390.0 30.6 %back.11 = (bf16[4096,4608]{1,0:T(8,128)(2,1)}, bf16[4,96,1536]{2,1,0:T(8,128)(2,1)}, bf16[288,768]{1,0:T(8,128)(2,1)}, bf16[96,1536]{1,0:T(8,128)(2,1)}, bf16[96,1536]{1,0:T(8,128)(2,1)}) custom-call(bf16[4096,768]{1,0:T(8,128)(2,1)} %get-tuple-element.58.refs_0_, ...), custom_call_target="tpu_custom_call", output_to_operand_aliasing={{0}: (5, {})} | custom-call | flops 14495514624 | bytes 129368064 | tf_op jit(solution)/shard_map/back/pallas_call | solution.py:231
  420.7 62.5 %input_back.3 = (bf16[4096,768]{1,0:T(8,128)(2,1)}, bf16[96,1536]{1,0:T(8,128)(2,1)}, bf16[96,1536]{1,0:T(8,128)(2,1)}, bf16[96,1536]{1,0:T(8,128)(2,1)}) custom-call(bf16[4096,4608]{1,0:T(8,128)(2,1)} %get-tuple-element.93.refs_0_, bf16[4096,768]{1,0:T(8,128)(2,1)} %bitcast.10, bf16[4096,768]{1,0:T(8,128)(2,1)} %get-tuple-element.78.refs_1_.refs_2_, ...), custom_call_target="tpu_custom_call" | custom-call | flops 28991029248 | bytes 57409536 | tf_op jit(solution)/shard_map/input_back/pallas_call | solution.py:231
  483.2 3.2 stack.1
  486.4 5.9 %copy.22 = bf16[1,4096,768]{2,1,0:T(8,128)(2,1)} copy(bf16[1,4096,768]{2,1,0:T(8,128)(2,1)} %bitcast.3) | data formatting | bytes 12582912
where the time goes:
time: 502 us; the launch traced here: 493 us
  Pallas kernels  486 us (97%)
  local copies, waits for them, and re-layouts  5.89 us (1%)
    pallas_call x12, Pallas kernels, call(): pl.pallas_call(body, grid=grid, in_specs=[spec(b, i) for _, b, i in all_i...  486 us

commit v1 on v0

--- a/solution.py
+++ b/solution.py
@@ -91,8 +91,9 @@
                 copy.start()
 
     def after(self, step, steps):
+        if step == steps - 2:
+            self.forward()
         if step == steps - 1:
-            self.forward()
             self.finish()
 
     def forward(self):
@@ -176,17 +177,19 @@
     def rows_of(chip, core):
         return acc[pl.ds(pl.multiple_of((chip * 2 + core) * rows, rows), rows), :]
 
+    copies = [
+        to_partner(src_ref=sent.at[chip], dst_ref=got.at[chip], send_sem=send.at[chip], recv_sem=recv.at[chip]) for chip in range(chips)
+    ]
     for chip in range(chips):
         sent[chip] = rows_of(chip, 1 - core).astype(BF)
-    copy = to_partner(src_ref=sent, dst_ref=got, send_sem=send, recv_sem=recv)
-    copy.start()
-    copy.wait()
+        copies[chip].start()
     for chip in range(chips):
+        copies[chip].wait()
         sums_ref[chip] = (rows_of(chip, core) + got[chip].astype(F32)).astype(BF)
 
 
 def pair_scratch(rows, n):
-    return [pltpu.VMEM((4, rows, n), BF)] * 2 + [DMA, DMA]
+    return [pltpu.VMEM((4, rows, n), BF)] * 2 + [DMA((4,))] * 2
 
 
 def call(kernel, grid, ins, outs, scratch, flops, number, moves=(), aliases=None, steered=False, name=None):
@@ -222,7 +225,7 @@
                     for m in moves:
                         getattr(m, do)(step, grid[0])
 
-        steps = sorted({0, grid[0] - 1} | {when for m in moves for _, when in getattr(m, "stages", ()) if when is not None})
+        steps = sorted({0, grid[0] - 2, grid[0] - 1} | {when for m in moves for _, when in getattr(m, "stages", ()) if when is not None})
         at_steps("before")
         kernel(*ins_[:n_in], *outs_[:n_out], *scratch_[:n_scratch])
         at_steps("after")
@@ -271,6 +274,12 @@
             def _():
                 move.forward()
 
+        if i == nc + 1:
+
+            @pl.when((c == nc) & (t == nt - late))
+            def _():
+                move.forward()
+
         if i <= nc:
 
             @pl.when((c == i) & (t == 0))
@@ -303,8 +312,7 @@
 
         @pl.when(t == nt - 1)
         def _():
-            for move in moves[nc + 1 :]:
-                move.forward()
+            moves[-1].forward()
             for move in moves[nc + 1 :]:
                 move.finish()
 
@@ -323,19 +331,22 @@
     def _():
         acc[...] = jnp.zeros_like(acc)
 
-    a, dh = a_ref[...], dh_ref[...]
-    if saved:
-        gate, up = given[0][...], given[1][...]
-    else:
-        gate, up = dot(a, given[0][:, :CB]), dot(a, given[0][:, CB:])
-    dp = dot(dh, wd_ref[...], NT).astype(BF).astype(F32)
-    sig = jax.nn.sigmoid(gate)
-    silu = gate * sig
-    d_ref[:, :CB] = (dp * up * (sig + silu * (1 - sig))).astype(BF)
-    d_ref[:, CB:] = (dp * silu).astype(BF)
-    if not saved:
-        p_ref[...] = (silu * up).astype(BF)
-    acc[...] += dot(a, d_ref[...], TN)
+    part = TB // 2 if saved else TB
+    for i in range(0, TB, part):
+        rows = slice(i, i + part)
+        a = a_ref[rows, :]
+        if saved:
+            gate, up = given[0][rows, :], given[1][rows, :]
+        else:
+            gate, up = dot(a, given[0][:, :CB]), dot(a, given[0][:, CB:])
+        dp = dot(dh_ref[rows, :], wd_ref[...], NT).astype(BF).astype(F32)
+        sig = jax.nn.sigmoid(gate)
+        silu = gate * sig
+        d_ref[rows, :CB] = (dp * up * (sig + silu * (1 - sig))).astype(BF)
+        d_ref[rows, CB:] = (dp * silu).astype(BF)
+        if not saved:
+            p_ref[rows, :] = (silu * up).astype(BF)
+    acc[...] += dot(a_ref[...], d_ref[...], TN)
 
     @pl.when(t == pl.num_programs(0) - 1)
     def _():
@@ -478,13 +489,9 @@
         dh1, t22, u2d = input_back(dgu2, h1, dy, [gu2_0, gu2_1, gu2_2], [Reduce(u22, (0, 3), (1, None)), Reduce(s2d, ("chips", None))])
         s1d, v2d = down_back(p1, dh1, [Reduce(u2d, (0, None))])
         so_far, s10, (t2d, u1d) = back(0, a1, dh1, wd1, [], [Reduce(v2d, (1, None)), Reduce(s1d, ("chips", None))])
-        so_far, s11, (v1d, u10) = back(1, a1, dh1, wd1, so_far, [Reduce(u1d, (0, None)), Reduce(s10, ("chips", None))])
-        (dgu1,), s12, (t1d, v10, u11) = back(
-            2, a1, dh1, wd1, so_far, [Reduce(v1d, (1, None)), Reduce(u10, (0, None)), Reduce(s11, ("chips", None))]
-        )
-        dx, t10, t11, t12 = input_back(
-            dgu1, x, dh1, gu1, [Reduce(v10, (1, None)), Reduce(u11, (0, 2), (1, None)), Reduce(s12, ("chips", 3), (0, 5), (1, None))]
-        )
+        so_far, s11, (t1d, u10) = back(1, a1, dh1, wd1, so_far, [Reduce(u1d, (0, 2), (1, None)), Reduce(s10, ("chips", None))])
+        (dgu1,), s12, (t10, u11) = back(2, a1, dh1, wd1, so_far, [Reduce(u10, (0, 2), (1, None)), Reduce(s11, ("chips", None))])
+        dx, t11, t12 = input_back(dgu1, x, dh1, gu1, [Reduce(u11, (0, 2), (1, None)), Reduce(s12, ("chips", 3), (0, 5), (1, None))])
 
         w_out = [((layers, rows_d, ff), BF)] * 2 + [((layers, rows_f, d), BF)]
         terms = (t10, t11, t12, t20, t21, t22, t1d, t2d)

time: 502 us -> 503 us (level)
  no operation moved by 1% of the time
where the time goes in v1:
time: 503 us; the launch traced here: 496 us
  Pallas kernels  489 us (97%)
  local copies, waits for them, and re-layouts  5.89 us (1%)
    pallas_call x12, Pallas kernels, call(): pl.pallas_call(body, grid=grid, in_specs=[spec(b, i) for _, b, i in all_i...  489 us

profile of v1, /device:TPU:0, one launch (start us, length us, event | category | flops | bytes accessed | tf_op | source)
XLA Modules:
  0.0 496.2 jit_solution(1102162965197599905)
XLA Ops:
  0.6 108.3 %fwd.1 = (f32[4096,2304]{1,0:T(8,128)}, f32[4096,2304]{1,0:T(8,128)}, bf16[4096,2304]{1,0:T(8,128)(2,1)}, bf16[4096,768]{1,0:T(8,128)(2,1)}, bf16[4096,768]{1,0:...) custom-call(bf16[4096,768]{1,0:T(8,128)(2,1)} %bitcast.9, ...), custom_call_target="tpu_custom_call" | custom-call | flops 43486543872 | bytes 6291456 | tf_op jit(solution)/shard_map/fwd/pallas_call | solution.py:234
  108.9 42.5 %back.6 = (bf16[4096,4608]{1,0:T(8,128)(2,1)}, bf16[4096,2304]{1,0:T(8,128)(2,1)}, bf16[4,96,1536]{2,1,0:T(8,128)(2,1)}, bf16[768,1536]{1,0:T(8,128)(2,1)}, bf16[768,1536]{1,0:T(8,128)(2,1)}) custom-call(bf16[4096,768]{1,0:T(8,128)(2,1)} %get-tuple-element.57.refs_0_, bf16[4096,768]{1,0:T(8,128)(2,1)} %bitcast.4, ...), custom_call_target="tpu_custom_call" | custom-call | flops 24159191040 | bytes 18481152 | tf_op jit(solution)/shard_map/back/pallas_call | solution.py:234
  151.4 37.9 %back.7 = (bf16[4096,4608]{1,0:T(8,128)(2,1)}, bf16[4096,2304]{1,0:T(8,128)(2,1)}, bf16[4,96,1536]{2,1,0:T(8,128)(2,1)}, bf16[96,1536]{1,0:T(8,128)(2,1)}) custom-call(bf16[4096,768]{1,0:T(8,128)(2,1)} %get-tuple-element.57.refs_0_, bf16[4096,768]{1,0:T(8,128)(2,1)} %bitcast.5, ...), custom_call_target="tpu_custom_call", output_to_operand_aliasing={{0}: (4, {}), {1}: (5, {})} | custom-call | flops 24159191040 | bytes 75104256 | tf_op jit(solution)/shard_map/back/pallas_call | solution.py:234
  189.3 38.5 %back.8 = (bf16[4096,4608]{1,0:T(8,128)(2,1)}, bf16[4096,2304]{1,0:T(8,128)(2,1)}, bf16[4,96,1536]{2,1,0:T(8,128)(2,1)}, bf16[96,1536]{1,0:T(8,128)(2,1)}, bf16[96,1536]{1,0:T(8,128)(2,1)}) custom-call(bf16[4096,768]{1,0:T(8,128)(2,1)} %get-tuple-element.57.refs_0_, bf16[4096,768]{1,0:T(8,128)(2,1)} %bitcast.6, ...), custom_call_target="tpu_custom_call", output_to_operand_aliasing={{0}: (4, {}), {1}: (5, {})} | custom-call | flops 24159191040 | bytes 75104256 | tf_op jit(solution)/shard_map/back/pallas_call | solution.py:234
  227.8 29.9 %down_back.2 = (bf16[4,288,768]{2,1,0:T(8,128)(2,1)}, bf16[96,1536]{1,0:T(8,128)(2,1)}, bf16[96,1536]{1,0:T(8,128)(2,1)}) custom-call(bf16[4096,2304]{1,0:T(8,128)(2,1)} %get-tuple-element.71.refs_0_, bf16[4096,768]{1,0:T(8,128)(2,1)} %bitcast.7, bf16[96,1536]{1,0:T(8,128)(2,1)} %get-tuple-element.72.refs_2_, bf16[4,96,1536]{2,1,0:T(8,128)(2,1)} %get-tuple-element.73.refs_3_), custom_call_target="tpu_custom_call" | custom-call | flops 14495514624 | bytes 25165824 | tf_op jit(solution)/shard_map/down_back/pallas_call | solution.py:234
  257.8 42.5 %input_back.2 = (bf16[4096,768]{1,0:T(8,128)(2,1)}, bf16[96,1536]{1,0:T(8,128)(2,1)}, bf16[288,768]{1,0:T(8,128)(2,1)}) custom-call(bf16[4096,4608]{1,0:T(8,128)(2,1)} %get-tuple-element.69.refs_0_, bf16[4096,768]{1,0:T(8,128)(2,1)} %get-tuple-element.70.refs_1_, bf16[4096,768]{1,0:T(8,128)(2,1)} %bitcast.8, bf16[768,1536]{1,0:T(8,128)(2,1)} %get-tuple-element.59.refs_3_, ...), custom_call_target="tpu_custom_call" | custom-call | flops 28991029248 | bytes 57409536 | tf_op jit(solution)/shard_map/input_back/pallas_call | solution.py:234
  300.3 25.2 %down_back.3 = (bf16[4,288,768]{2,1,0:T(8,128)(2,1)}, bf16[288,768]{1,0:T(8,128)(2,1)}) custom-call(bf16[4096,2304]{1,0:T(8,128)(2,1)} %get-tuple-element.80.refs_0_, bf16[4096,768]{1,0:T(8,128)(2,1)} %get-tuple-element.76.refs_1_.refs_2_, bf16[288,768]{1,0:T(8,128)(2,1)} %get-tuple-element.81.refs_2_), custom_call_target="tpu_custom_call" | custom-call | flops 14495514624 | bytes 25165824 | tf_op jit(solution)/shard_map/down_back/pallas_call | solution.py:234
  325.5 30.5 %back.9 = (bf16[4096,4608]{1,0:T(8,128)(2,1)}, bf16[4,96,1536]{2,1,0:T(8,128)(2,1)}, bf16[288,768]{1,0:T(8,128)(2,1)}, bf16[288,768]{1,0:T(8,128)(2,1)}) custom-call(bf16[4096,768]{1,0:T(8,128)(2,1)} %get-tuple-element.56.refs_0_, bf16[4096,768]{1,0:T(8,128)(2,1)} %get-tuple-element.76.refs_1_.refs_2_, bf16[2304,768]{1,0:T(8,128)(2,1)} %get-tuple-element.77.refs_2_, ...), custom_call_target="tpu_custom_call" | custom-call | flops 14495514624 | bytes 91619328 | tf_op jit(solution)/shard_map/back/pallas_call | solution.py:234
  356.0 41.0 %back.10 = (bf16[4096,4608]{1,0:T(8,128)(2,1)}, bf16[4,96,1536]{2,1,0:T(8,128)(2,1)}, bf16[288,768]{1,0:T(8,128)(2,1)}, bf16[96,1536]{1,0:T(8,128)(2,1)}) custom-call(bf16[4096,768]{1,0:T(8,128)(2,1)} %get-tuple-element.56.refs_0_, bf16[4096,768]{1,0:T(8,128)(2,1)} %get-tuple-element.76.refs_1_.refs_2_, ...), custom_call_target="tpu_custom_call", output_to_operand_aliasing={{0}: (5, {})} | custom-call | flops 14495514624 | bytes 129368064 | tf_op jit(solution)/shard_map/back/pallas_call | solution.py:234
  397.0 31.8 %back.11 = (bf16[4096,4608]{1,0:T(8,128)(2,1)}, bf16[4,96,1536]{2,1,0:T(8,128)(2,1)}, bf16[96,1536]{1,0:T(8,128)(2,1)}, bf16[96,1536]{1,0:T(8,128)(2,1)}) custom-call(bf16[4096,768]{1,0:T(8,128)(2,1)} %get-tuple-element.56.refs_0_, bf16[4096,768]{1,0:T(8,128)(2,1)} %get-tuple-element.76.refs_1_.refs_2_, ...), custom_call_target="tpu_custom_call", output_to_operand_aliasing={{0}: (5, {})} | custom-call | flops 14495514624 | bytes 129368064 | tf_op jit(solution)/shard_map/back/pallas_call | solution.py:234
  428.8 57.8 %input_back.3 = (bf16[4096,768]{1,0:T(8,128)(2,1)}, bf16[96,1536]{1,0:T(8,128)(2,1)}, bf16[96,1536]{1,0:T(8,128)(2,1)}) custom-call(bf16[4096,4608]{1,0:T(8,128)(2,1)} %get-tuple-element.90.refs_0_, bf16[4096,768]{1,0:T(8,128)(2,1)} %bitcast.10, bf16[4096,768]{1,0:T(8,128)(2,1)} %get-tuple-element.76.refs_1_.refs_2_, ...), custom_call_target="tpu_custom_call" | custom-call | flops 28991029248 | bytes 57409536 | tf_op jit(solution)/shard_map/input_back/pallas_call | solution.py:234
  486.6 3.2 stack.1
  489.8 5.9 %copy.22 = bf16[1,4096,768]{2,1,0:T(8,128)(2,1)} copy(bf16[1,4096,768]{2,1,0:T(8,128)(2,1)} %bitcast.3) | data formatting | bytes 12582912
